TPU v7x, 256 devices: a whole 4x4x8 slice. The times are simulated.
256 devices in a mesh: group: 32 (over x, y, core), inst: 8 (over z).
Axes of the slice: x: 4, y: 4, z: 8, core: 2. Of those that a mesh axis runs over, the one named last changes fastest.
Arguments:
- old_cache: bfloat16 [8, 2048, 16, 2048], P('inst', 'group'), may hold values from -64 to 64, as said below
- block_table: int32 [128, 128], replicated, may hold values from 0 to 2047, as said below
- place_after: int32 [128], replicated, may hold values from 0 to 127, as said below
- context_len: int32 [128], replicated, may hold values from 256 to 2048
- queries: bfloat16 [32768, 4096], P(('group', 'inst')), may hold values from -64 to 64
- new_kv: bfloat16 [32768, 2048], P(('group', 'inst')), may hold values from -6 to 6
Outputs:
- attended: bfloat16 [32768, 4096], P(('group', 'inst'))
Inputs may be any that keep to these rules, and one draw needn't show every extreme that they name: Each of old_cache and queries lies within the printed range. A permutation: request r moves to group index place_after[r] // 4, as that group's request number place_after[r] % 4. block_table[r, k] lies on the devices of inst index k // 16: on group index block_table[r, k] // 64, slot block_table[r, k] % 64. Every slot of every device holds exactly one block, and each device holds exactly 2 blocks of the requests of each new group.
All inputs are finite; a program needn't handle non-finite values.
Results may differ from a plain program's by a relative error of at most 0.0075.
Values may be sent and summed in bfloat16 or wider, within the bound.
A program may use at most 128 MiB of HBM per device.

v0:
```python
import jax
import jax.numpy as jnp
from jax import lax
from jax.sharding import PartitionSpec as P

KVH = 8
HD = 128


NEG_FILL = -1e30


def swapped(array, axis, apart):
    return lax.ppermute(array, axis, [(i, i ^ 1 << apart) for i in range(lax.axis_size(axis))])


def absorb(carried, query_heads, keyvals, allowed):
    largest, total, summed = carried
    count = keyvals.shape[0]
    keys = keyvals[:, : KVH * HD].reshape(count, KVH, HD)
    values = keyvals[:, KVH * HD :].reshape(count, KVH, HD)
    scores = jnp.einsum(
        "qhgd,khd->hgqk", query_heads, keys, preferred_element_type=jnp.float32
    ) * HD ** (-0.5)
    scores = jnp.where(allowed[None, None], scores, -jnp.inf)
    updated = jnp.maximum(largest, jnp.max(scores, axis=-1))
    weights = jnp.exp(scores - updated[..., None]).astype(jnp.bfloat16)
    factor = jnp.exp(largest - updated)
    total = total * factor + jnp.sum(weights.astype(jnp.float32), axis=-1)
    summed = summed * factor[..., None] + jnp.einsum(
        "hgqk,khd->hgqd", weights, values, preferred_element_type=jnp.float32
    )
    return (updated, total, summed)


def combine(first, second):
    updated = jnp.maximum(first[0], second[0])
    left = jnp.exp(first[0] - updated)
    right = jnp.exp(second[0] - updated)
    total = first[1] * left + second[1] * right
    summed = first[2] * left[..., None] + second[2] * right[..., None]
    return (updated, total, summed)


def finish(carried):
    result = carried[2] / carried[1][..., None]
    count = result.shape[2]
    return jnp.transpose(result, (2, 0, 1, 3)).reshape(count, -1).astype(jnp.bfloat16)


def start_state(count, groups):
    return (
        jnp.full((KVH, groups, count), NEG_FILL, jnp.float32),
        jnp.zeros((KVH, groups, count), jnp.float32),
        jnp.zeros((KVH, groups, count, HD), jnp.float32),
    )


def sweep(carried, query_heads, cache, positions, length, block_width):
    live_total = jnp.sum((positions < length).astype(jnp.int32))
    rounds = (live_total + block_width - 1) // block_width

    def visit(number, state):
        begin = number * block_width
        piece = lax.dynamic_slice_in_dim(cache, begin, block_width, 0)
        spots = lax.dynamic_slice_in_dim(positions, begin, block_width, 0)
        allowed = jnp.broadcast_to((spots < length)[None, :], (query_heads.shape[0], block_width))
        return absorb(state, query_heads, piece, allowed)

    return lax.fori_loop(0, rounds, visit, carried)


def on_device(old_cache, block_table, place_after, context_len, queries, new_kv):
    ninst = lax.axis_size("inst")
    ngroup = lax.axis_size("group")
    group_index = lax.axis_index("group")
    inst_index = lax.axis_index("inst")
    slots = old_cache.shape[1]
    blk = old_cache.shape[2]
    width = old_cache.shape[3]
    reqs = place_after.shape[0]
    nblk = block_table.shape[1]
    per_inst = nblk // ninst
    per_pair = slots // ngroup
    rgroup = ninst // 2
    half = per_inst // 2
    local = old_cache[0]
    columns = lax.dynamic_slice_in_dim(block_table, inst_index * per_inst, per_inst, 1)
    owners = columns // slots
    target = place_after // rgroup
    within = place_after % rgroup
    block_ids = lax.broadcasted_iota(jnp.int32, (reqs, per_inst), 1)
    beyond = ngroup * slots + 1
    order_key = jnp.where(
        owners == group_index,
        target[:, None] * slots + within[:, None] * per_inst + block_ids,
        beyond,
    )
    picked = jnp.argsort(order_key.reshape(-1))[:slots]
    source_slot = columns.reshape(-1)[picked] % slots
    outgoing = local[source_slot].reshape(ngroup, per_pair, blk, width)
    arrived = lax.all_to_all(outgoing, "group", split_axis=0, concat_axis=0, tiled=True)
    request_range = jnp.arange(reqs, dtype=jnp.int32)
    slot_ids = group_index * rgroup + jnp.arange(rgroup, dtype=jnp.int32)
    matched = place_after[None, :] == slot_ids[:, None]
    request_ids = jnp.sum(jnp.where(matched, request_range[None, :], 0), axis=1)
    source_of = columns[request_ids] // slots
    item_ids = jnp.arange(slots, dtype=jnp.int32)
    rank = jnp.argsort(jnp.argsort(source_of.reshape(-1) * slots + item_ids))
    dest_inst = item_ids // half
    item_of_dest = dest_inst // 2 * per_inst + 2 * (item_ids % half) + dest_inst % 2
    sectioned = arrived.reshape(slots, blk, width)[rank[item_of_dest]].reshape(
        ninst, half, blk, width
    )
    settled = lax.all_to_all(sectioned, "inst", split_axis=0, concat_axis=0, tiled=True).reshape(
        ninst * half * blk, width
    )
    parity = inst_index % 2
    own_request = request_ids[inst_index // 2]
    length = jnp.sum(jnp.where(request_range == own_request, context_len, 0))
    tokens = queries.shape[0]
    groups = queries.shape[1] // (KVH * HD)
    query_heads = queries.reshape(tokens, KVH, groups, HD)
    cache_len = settled.shape[0]
    block_width = min(512, cache_len)
    token_ids = jnp.arange(cache_len, dtype=jnp.int32)
    own_places = (2 * (token_ids // blk) + parity) * blk + token_ids % blk
    fresh_ids = jnp.arange(tokens, dtype=jnp.int32)
    own_new = parity * tokens + fresh_ids
    other_queries = swapped(queries, "inst", 0)
    joined = jnp.concatenate([query_heads, other_queries.reshape(tokens, KVH, groups, HD)], axis=0)
    joined_places = jnp.concatenate([own_new, (1 - parity) * tokens + fresh_ids])
    state = start_state(2 * tokens, groups)
    state = sweep(state, joined, settled, own_places, length, block_width)
    state = absorb(state, joined, new_kv, joined_places[:, None] >= own_new[None, :])
    mine = (state[0][:, :, :tokens], state[1][:, :, :tokens], state[2][:, :, :tokens])
    theirs = (state[0][:, :, tokens:], state[1][:, :, tokens:], state[2][:, :, tokens:])
    returned = swapped((theirs[0], theirs[1], theirs[2]), "inst", 0)
    return finish(combine(mine, returned))


def solution(mesh):
    return jax.shard_map(
        on_device,
        mesh=mesh,
        in_specs=(
            P("inst", "group", None, None),
            P(),
            P(),
            P(),
            P(("group", "inst"), None),
            P(("group", "inst"), None),
        ),
        out_specs=P(("group", "inst"), None),
        check_vma=False,
    )
```

profile of v0, /device:TPU:6, one launch (start us, length us, event | category | flops | bytes accessed | tf_op | source)
XLA Modules:
  0.0 324.7 jit_solution(17661359405260655513)
XLA Ops:
  0.0 0.7 fusion.31
  0.7 1.0 add_select_fusion.1
  1.8 5.0 %sort.48 = (s32[2048]{0:T(1024)}, s32[2048]{0:T(1024)S(1)}) sort(s32[2048]{0:T(1024)S(1)} %reshape.293, s32[2048]{0:T(1024)S(1)} %iota.49), dimensions={0}, to_apply=%region_3.4 | sort | flops 22528 | bytes 32768 | tf_op jit(solution)/shard_map/jit(argsort)/sort | solution.py:99
  6.9 0.8 gather_fusion
  7.6 4.9 %gather_fusion.1 = bf16[64,16,2048]{2,1,0:T(8,128)(2,1)} fusion(bf16[64,16,2048]{2,1,0:T(8,128)(2,1)} %bitcast.118, s32[1024]{0:T(1024)S(1)} %pad_clamp_fusion.3), kind=kCustom, calls=%fused_computation.1 | custom fusion | bytes 8388864 | tf_op jit(solution)/shard_map/gather | solution.py:101
  12.6 7.8 %all-to-all-start = ((bf16[32,2,16,2048]{3,2,1,0:T(8,128)(2,1)}), bf16[32,2,16,2048]{3,2,1,0:T(8,128)(2,1)}, u32[]{:S(2)}, u32[]{:S(2)}) async-start(bf16[32,2,16,2048]{3,2,1,0:T(8,128)(2,1)} %bitcast.113), calls=%async_computation | async-start | bytes 8388608 | tf_op jit(solution)/shard_map/all_to_all | solution.py:102
  21.3 2.0 sort.49
  23.3 2.0 sort.50
  25.4 0.8 gather_fusion.3
  26.2 45.0 %all-to-all-done = bf16[32,2,16,2048]{3,2,1,0:T(8,128)(2,1)} async-done(((bf16[32,2,16,2048]{3,2,1,0:T(8,128)(2,1)}), bf16[32,2,16,2048]{3,2,1,0:T(8,128)(2,1)}, u32[]{:S(2)}, u32[]{:S(2)}) %all-to-all-start) | async-done | bytes 4194336 | tf_op jit(solution)/shard_map/all_to_all | solution.py:102
  71.1 4.9 %gather_fusion.4 = bf16[64,16,2048]{2,1,0:T(8,128)(2,1)} fusion(bf16[64,16,2048]{2,1,0:T(8,128)(2,1)} %bitcast.10, s32[1024]{0:T(1024)S(1)} %pad_clamp_fusion), kind=kCustom, calls=%fused_computation.4 | custom fusion | bytes 8388864 | tf_op jit(solution)/shard_map/gather | solution.py:112
  76.1 8.6 %all-to-all-start.1 = ((bf16[8,8,16,2048]{3,2,1,0:T(8,128)(2,1)}), bf16[8,8,16,2048]{3,2,1,0:T(8,128)(2,1)}, u32[]{:S(2)}, u32[]{:S(2)}) async-start(bf16[8,8,16,2048]{3,2,1,0:T(8,128)(2,1)} %bitcast.112), calls=%async_computation.1 | async-start | bytes 8388608 | tf_op jit(solution)/shard_map/all_to_all | solution.py:115
  85.3 2.1 collective-permute-start
  88.0 1.3 fusion.29
  89.3 1.3 convert_reduce_fusion.2
  91.2 0.7 copy.44
  91.9 1.8 fusion.43
  93.7 0.8 copy.66
  94.5 1.1 copy.50
  95.8 103.3 %collective-permute-done = bf16[128,4096]{0,1:T(8,128)(2,1)S(1)} collective-permute-done((bf16[128,4096]{0,1:T(8,128)(2,1)S(1)}, bf16[128,4096]{0,1:T(8,128)(2,1)S(1)}, u32[]{:S(2)}, u32[]{:S(2)}) %collective-permute-start) | collective-permute-done | bytes 1048608 | tf_op jit(solution)/shard_map/ppermute | solution.py:14
  199.1 1.3 copy.45
  200.4 1.5 pad_maximum_fusion
  202.0 3.3 %bitcast_reduce_fusion.1 = (f32[8,4,256]{2,1,0:T(4,128)}, f32[8,256,4,128]{1,3,2,0:T(8,128)}) fusion(pred[256,128]{0,1:T(8,128)(4,1)S(1)} %broadcast_compare_fusion, bf16[128,8,128,1]{0,2,3,1:T(8,128)(2,1)S(1)} %bitcast.128, bf16[128,8,4,128]{3,0,2,1:T(8,128)(2,1)S(1)} %copy-done.3, bf16[128,8,4,128]{3,0,2,1:T(8,128)(2,1)S(1)} %copy.44), kind=kOutput, calls=%fused_computation.17 | convolution fusion | flops 275767296 | bytes 6619136 | tf_op jit(solution)/shard_map/qhgd,khd->hgqk/dot_general | solution.py:22
  205.3 2.5 broadcast_in_dim.60
  207.7 55.6 %while.14 = (s32[]{:T(128)}, f32[8,4,256]{2,1,0:T(4,128)S(1)}, f32[8,4,256]{2,1,0:T(4,128)S(1)}, f32[8,4,256,128]{3,2,1,0:T(8,128)}, s32[]{:T(128)}, /*index=5*/...) while((s32[]{:T(128)}, f32[8,4,256]{2,1,0:T(4,128)S(1)}, ...), condition=%wide.region_9.10_spmd, body=%wide.region_6.9_spmd.sunk | while | flops 2204123648 | bytes 143134992 | solution.py:70
  207.9 0.7 dynamic-slice_compare_fusion.2
  208.6 3.0 fusion.58
  211.7 1.5 copy.71
  213.2 3.9 %bitcast_reduce_fusion.3 = (f32[8,4,256]{2,1,0:T(4,128)S(1)}, f32[8,512,256,4]{2,1,3,0:T(8,128)S(1)}) fusion(pred[512]{0:T(512)(128)(4,1)S(1)} %dynamic-slice_compare_fusion.2, bf16[512,8,128,1]{0,2,3,1:T(8,128)(2,1)S(1)} %bitcast.110, bf16[256,8,4,128]{3,0,2,1:T(8,128)(2,1)S(1)} %get-tuple-element.227), kind=kOutput, calls=%fused_computation.6.clone.1 | convolution fusion | flops 1086316544 | bytes 19956224 | tf_op jit(solution)/shard_map/while/body/qhgd,khd->hgqk/dot_general | solution.py:22
  217.2 4.0 %convert_reduce_fusion.4 = f32[8,4,256]{2,1,0:T(4,128)S(1)} fusion(f32[8,4,256]{2,1,0:T(4,128)S(1)} %max.20, f32[8,512,256,4]{2,1,3,0:T(8,128)S(1)} %get-tuple-element.187, pred[512]{0:T(512)(128)(4,1)S(1)} %dynamic-slice_compare_fusion.2), kind=kLoop, calls=%fused_computation.9.clone.1 | loop fusion | flops 25157632 | bytes 16843264 | tf_op jit(solution)/shard_map/while/body/reduce_sum | solution.py:29
  221.2 1.8 copy-done
  223.1 1.3 copy.72
  224.4 11.2 %multiply_add_fusion.7 = f32[8,4,256,128]{3,2,1,0:T(8,128)} fusion(f32[8,4,256,128]{3,2,1,0:T(8,128)} %get-tuple-element.208, bf16[512,8,128,1]{0,2,3,1:T(8,128)(2,1)} %bitcast.111, f32[8,4,256]{2,1,0:T(4,128)S(1)} %bitcast.127, f32[8,512,256,4]{2,1,3,0:T(8,128)} %copy-done, f32[8,4,256]{2,1,0:T(4,128)S(1)} %max.20, ...), kind=kOutput, calls=%fused_computation.11.clone.1 | convolution fusion | flops 1092616192 | bytes 26280448 | tf_op jit(solution)/shard_map/while/body/hgqk,khd->hgqd/dot_general | solution.py:30
  235.6 0.7 dynamic-slice_compare_fusion.2
  236.3 3.0 fusion.58
  239.4 1.5 copy.71
  240.9 3.9 %bitcast_reduce_fusion.3 = (f32[8,4,256]{2,1,0:T(4,128)S(1)}, f32[8,512,256,4]{2,1,3,0:T(8,128)S(1)}) fusion(pred[512]{0:T(512)(128)(4,1)S(1)} %dynamic-slice_compare_fusion.2, bf16[512,8,128,1]{0,2,3,1:T(8,128)(2,1)S(1)} %bitcast.110, bf16[256,8,4,128]{3,0,2,1:T(8,128)(2,1)S(1)} %get-tuple-element.227), kind=kOutput, calls=%fused_computation.6.clone.1 | convolution fusion | flops 1086316544 | bytes 19956224 | tf_op jit(solution)/shard_map/while/body/qhgd,khd->hgqk/dot_general | solution.py:22
  244.9 4.0 %convert_reduce_fusion.4 = f32[8,4,256]{2,1,0:T(4,128)S(1)} fusion(f32[8,4,256]{2,1,0:T(4,128)S(1)} %max.20, f32[8,512,256,4]{2,1,3,0:T(8,128)S(1)} %get-tuple-element.187, pred[512]{0:T(512)(128)(4,1)S(1)} %dynamic-slice_compare_fusion.2), kind=kLoop, calls=%fused_computation.9.clone.1 | loop fusion | flops 25157632 | bytes 16843264 | tf_op jit(solution)/shard_map/while/body/reduce_sum | solution.py:29
  248.9 1.8 copy-done
  250.8 1.3 copy.72
  252.1 11.2 %multiply_add_fusion.7 = f32[8,4,256,128]{3,2,1,0:T(8,128)} fusion(f32[8,4,256,128]{3,2,1,0:T(8,128)} %get-tuple-element.208, bf16[512,8,128,1]{0,2,3,1:T(8,128)(2,1)} %bitcast.111, f32[8,4,256]{2,1,0:T(4,128)S(1)} %bitcast.127, f32[8,512,256,4]{2,1,3,0:T(8,128)} %copy-done, f32[8,4,256]{2,1,0:T(4,128)S(1)} %max.20, ...), kind=kOutput, calls=%fused_computation.11.clone.1 | convolution fusion | flops 1092616192 | bytes 26280448 | tf_op jit(solution)/shard_map/while/body/hgqk,khd->hgqd/dot_general | solution.py:30
  263.3 5.4 %copy.49 = f32[8,4,256,128]{2,3,1,0:T(8,128)} copy(f32[8,4,256,128]{3,2,1,0:T(8,128)} %get-tuple-element.61) | data formatting | bytes 8388608 | tf_op jit(solution)/shard_map/while | solution.py:70
  268.7 3.3 %convert_reduce_fusion.1 = f32[8,4,256]{2,1,0:T(4,128)S(1)} fusion(f32[8,4,256]{2,1,0:T(4,128)S(1)} %max.9, f32[8,256,4,128]{1,3,2,0:T(8,128)} %get-tuple-element.116, pred[256,128]{0,1:T(8,128)(4,1)S(1)} %copy-done.6), kind=kLoop, calls=%fused_computation.20 | loop fusion | flops 6283264 | bytes 4292608 | tf_op jit(solution)/shard_map/reduce_sum | solution.py:29
  272.2 3.7 %multiply_add_fusion.2 = f32[8,4,256,128]{2,3,1,0:T(8,128)S(1)} fusion(f32[8,4,256,128]{2,3,1,0:T(8,128)} %copy.49, bf16[128,8,128,1]{0,2,3,1:T(8,128)(2,1)S(1)} %bitcast.124, f32[8,4,256]{2,1,0:T(4,128)S(1)} %bitcast.129, f32[8,256,4,128]{1,3,2,0:T(8,128)S(1)} %copy-done.2, f32[8,4,256]{2,1,0:T(4,128)S(1)} %max.9, pred[256,128]{0,1:T(8,128)(4,1)S(1)} %copy-done.6), kind=kOutput, calls=%fused_computation.21 | convolution fusion | flops 274726912 | bytes 12943360 | tf_op jit(solution)/shard_map/hgqk,khd->hgqd/dot_general | solution.py:30
  276.0 0.7 collective-permute-start.2
  276.8 1.5 collective-permute-start.3
  278.9 43.7 %collective-permute-done.3 = f32[8,4,128]{2,1,0:T(4,128)S(1)} collective-permute-done((f32[8,4,128]{2,1,0:T(4,128)S(1)}, f32[8,4,128]{2,1,0:T(4,128)S(1)}, u32[]{:S(2)}, u32[]{:S(2)}) %collective-permute-start.3) | collective-permute-done | bytes 16416 | tf_op jit(solution)/shard_map/ppermute | solution.py:14
  323.4 1.3 copy.52
  (70 shorter events, 4.4 us)
Async XLA Ops:
  12.6 7.8 %copy-start.9 = (s32[128]{0:T(128)S(1)}, s32[128]{0:T(128)}, u32[]{:S(2)}) copy-start(s32[128]{0:T(128)} %param.10) | copy-start | bytes 1540
  12.6 58.6 %all-to-all-start = ((bf16[32,2,16,2048]{3,2,1,0:T(8,128)(2,1)}), bf16[32,2,16,2048]{3,2,1,0:T(8,128)(2,1)}, u32[]{:S(2)}, u32[]{:S(2)}) async-start(bf16[32,2,16,2048]{3,2,1,0:T(8,128)(2,1)} %bitcast.113), calls=%async_computation | async-start | bytes 8388608 | tf_op jit(solution)/shard_map/all_to_all | solution.py:102
  76.1 8.6 %copy-start.4 = (bf16[128,4096]{1,0:T(8,128)(2,1)S(1)}, bf16[128,4096]{1,0:T(8,128)(2,1)}, u32[]{:S(2)}) copy-start(bf16[128,4096]{1,0:T(8,128)(2,1)} %param.12) | copy-start | bytes 3145732
  76.1 12.0 %copy-start.10 = (s32[128]{0:T(128)S(1)}, s32[128]{0:T(128)}, u32[]{:S(2)}) copy-start(s32[128]{0:T(128)} %param.11) | copy-start | bytes 1540
  76.1 129.2 %all-to-all-start.1 = ((bf16[8,8,16,2048]{3,2,1,0:T(8,128)(2,1)}), bf16[8,8,16,2048]{3,2,1,0:T(8,128)(2,1)}, u32[]{:S(2)}, u32[]{:S(2)}) async-start(bf16[8,8,16,2048]{3,2,1,0:T(8,128)(2,1)} %bitcast.112), calls=%async_computation.1 | async-start | bytes 8388608 | tf_op jit(solution)/shard_map/all_to_all | solution.py:115
  85.3 113.7 %collective-permute-start = (bf16[128,4096]{0,1:T(8,128)(2,1)S(1)}, bf16[128,4096]{0,1:T(8,128)(2,1)S(1)}, u32[]{:S(2)}, u32[]{:S(2)}) collective-permute-start(bf16[128,4096]{0,1:T(8,128)(2,1)S(1)} %copy.42), channel_id=1, source_target_pairs={{0,1},{1,0},{2,3},{3,2},{4,5},{5,4},{6,7},{7,6},{8,9},{9,8},{10,11... | collective-permute-start | bytes 3145736 | tf_op jit(solution)/shard_map/ppermute | solution.py:14
  95.8 109.5 %copy-start.5 = (pred[256,128]{0,1:T(8,128)(4,1)}, pred[256,128]{0,1:T(8,128)(4,1)S(1)}, u32[]{:S(2)}) copy-start(pred[256,128]{0,1:T(8,128)(4,1)S(1)} %broadcast_compare_fusion) | copy-start | bytes 98308
  200.4 1.5 copy-start.3
  200.4 1.6 copy-start.7
  217.1 5.9 %copy-start = (f32[8,512,256,4]{2,1,3,0:T(8,128)}, f32[8,512,256,4]{2,1,3,0:T(8,128)S(1)}, u32[]{:S(2)}) copy-start(f32[8,512,256,4]{2,1,3,0:T(8,128)S(1)} %get-tuple-element.187) | copy-start | bytes 50331652 | tf_op jit(solution)/shard_map/while
  217.2 5.9 %copy-start.1 = (bf16[512,1024]{1,0:T(8,128)(2,1)S(1)}, bf16[512,1024]{1,0:T(8,128)(2,1)}, u32[]{:S(2)}) copy-start(bf16[512,1024]{1,0:T(8,128)(2,1)} %get-tuple-element.190) | copy-start | bytes 3145732 | tf_op jit(solution)/shard_map/while
  244.8 5.9 %copy-start = (f32[8,512,256,4]{2,1,3,0:T(8,128)}, f32[8,512,256,4]{2,1,3,0:T(8,128)S(1)}, u32[]{:S(2)}) copy-start(f32[8,512,256,4]{2,1,3,0:T(8,128)S(1)} %get-tuple-element.187) | copy-start | bytes 50331652 | tf_op jit(solution)/shard_map/while
  244.8 5.9 %copy-start.1 = (bf16[512,1024]{1,0:T(8,128)(2,1)S(1)}, bf16[512,1024]{1,0:T(8,128)(2,1)}, u32[]{:S(2)}) copy-start(bf16[512,1024]{1,0:T(8,128)(2,1)} %get-tuple-element.190) | copy-start | bytes 3145732 | tf_op jit(solution)/shard_map/while
  263.3 5.4 %copy-start.8 = (f32[8,4,256]{2,1,0:T(4,128)S(1)}, f32[8,4,256]{2,1,0:T(4,128)}, u32[]{:S(2)}) copy-start(f32[8,4,256]{2,1,0:T(4,128)} %get-tuple-element.115) | copy-start | bytes 98308
  263.3 5.4 %copy-start.6 = (pred[256,128]{0,1:T(8,128)(4,1)S(1)}, pred[256,128]{0,1:T(8,128)(4,1)}, u32[]{:S(2)}) copy-start(pred[256,128]{0,1:T(8,128)(4,1)} %copy-done.5) | copy-start | bytes 98308
  268.7 3.4 %copy-start.2 = (f32[8,256,4,128]{1,3,2,0:T(8,128)S(1)}, f32[8,256,4,128]{1,3,2,0:T(8,128)}, u32[]{:S(2)}) copy-start(f32[8,256,4,128]{1,3,2,0:T(8,128)} %get-tuple-element.116) | copy-start | bytes 12582916
  276.0 46.7 %collective-permute-start.2 = (f32[8,4,128,128]{2,3,1,0:T(8,128)S(1)}, f32[8,4,128,128]{2,3,1,0:T(8,128)S(1)}, u32[]{:S(2)}, u32[]{:S(2)}) collective-permute-start(f32[8,4,128,128]{2,3,1,0:T(8,128)S(1)} %slice.55), channel_id=1, source_target_pairs={{0,1},{1,0},{2,3},{3,2},{4,5},{5,4},{6,7},{7,6},{8,9},{9,8},{10,11... | collective-permute-start | bytes 6291464 | tf_op jit(solution)/shard_map/ppermute | solution.py:14
  276.8 45.8 %collective-permute-start.3 = (f32[8,4,128]{2,1,0:T(4,128)S(1)}, f32[8,4,128]{2,1,0:T(4,128)S(1)}, u32[]{:S(2)}, u32[]{:S(2)}) collective-permute-start(f32[8,4,128]{2,1,0:T(4,128)S(1)} %slice.57), channel_id=1, source_target_pairs={{0,1},{1,0},{2,3},{3,2},{4,5},{5,4},{6,7},{7,6},{8,9},{9,8},{10,11... | collective-permute-start | bytes 49160 | tf_op jit(solution)/shard_map/ppermute | solution.py:14
  278.2 44.5 %collective-permute-start.1 = (f32[8,4,128]{2,1,0:T(4,128)S(1)}, f32[8,4,128]{2,1,0:T(4,128)S(1)}, u32[]{:S(2)}, u32[]{:S(2)}) collective-permute-start(f32[8,4,128]{2,1,0:T(4,128)S(1)} %slice.54), channel_id=1, source_target_pairs={{0,1},{1,0},{2,3},{3,2},{4,5},{5,4},{6,7},{7,6},{8,9},{9,8},{10,11... | collective-permute-start | bytes 49160 | tf_op jit(solution)/shard_map/ppermute | solution.py:14
where the time goes:
time: 327 us; the launch traced here: 325 us
  waiting for transfers between devices  192 us (59%)
  local copies, waits for them, and re-layouts  44.1 us (13%)
  matrix products  37.3 us (11%)
  other arithmetic  28.6 us (9%)
  starting transfers between devices  21.3 us (7%)
    ppermute x4, waiting for transfers between devices, swapped(): lax.ppermute(array, axis, [(i, i ^ 1 << apart) for i in range(lax.axis_si...  147 us
    all_to_all x1, waiting for transfers between devices, on_device(): lax.all_to_all(outgoing, 'group', split_axis=0, concat_axis=0, tiled=True)  45 us
    dot_general x3, matrix products, absorb(): jnp.einsum('hgqk,khd->hgqd', weights, values, preferred_element_type=jnp....  26.1 us
    reduce_sum x3, other arithmetic, absorb(): total = total * factor + jnp.sum(weights.astype(jnp.float32), axis=-1)  11.4 us
    dot_general x3, matrix products, absorb(): jnp.einsum('qhgd,khd->hgqk', query_heads, keys, preferred_element_type=jn...  11.2 us
    while x14, local copies, waits for them, and re-layouts  9.34 us
    all_to_all x1, starting transfers between devices, on_device(): lax.all_to_all(sectioned, 'inst', split_axis=0, concat_axis=0, tiled=True)  8.6 us
    all_to_all x1, starting transfers between devices, on_device(): lax.all_to_all(outgoing, 'group', split_axis=0, concat_axis=0, tiled=True)  7.79 us
  transfers between devices with their start and end apart: 6, of which 4 were waited for; matrix products, arithmetic and copies ran while one was open for 6% of the time, Pallas kernels for 0%

commit v1 on v0

v1 whole, which is shorter than its diff:
```python
import functools

import jax
import jax.numpy as jnp
from jax import lax
from jax.experimental import pallas as pl
from jax.experimental.pallas import tpu as pltpu
from jax.sharding import PartitionSpec as P

KVH = 8
HD = 128
NCH = 4
BIG = -1e30
MESH = pl.DeviceIdType.MESH


def tables(block_table, place_after, context_len, slots, per_inst):
    g = lax.axis_index("group")
    i = lax.axis_index("inst")
    ngroup = lax.axis_size("group")
    rgroup = slots // per_inst
    columns = lax.dynamic_slice_in_dim(block_table, i * per_inst, per_inst, 1)
    kk = lax.broadcasted_iota(jnp.int32, columns.shape, 1)
    keys = (place_after[:, None] * per_inst + kk).reshape(1, -1)
    places = columns.reshape(1, -1)
    ids = jnp.arange(slots, dtype=jnp.int32)
    mine = g * slots + ids
    key_of_slot = jnp.sum(jnp.where(places == mine[:, None], keys, 0), axis=1)
    rank = jnp.sum((key_of_slot[None, :] < key_of_slot[:, None]).astype(jnp.int32), axis=1)
    pos = (rank - g * (slots // ngroup) + slots) % slots
    send = jnp.sum(jnp.where(pos[None, :] == ids[:, None], ids[None, :], 0), axis=1)
    place_of_item = jnp.sum(jnp.where(keys == mine[:, None], places, 0), axis=1)
    owner = place_of_item // slots
    same = (owner[None, :] == owner[:, None]) & (ids[None, :] < ids[:, None])
    second = jnp.sum(same.astype(jnp.int32), axis=1)
    recv = ((g - owner + ngroup) % ngroup) * (slots // ngroup) + second
    slot = g * rgroup + i // 2
    length = jnp.sum(jnp.where(place_after == slot, context_len, 0))
    return jnp.concatenate([send, recv, jnp.broadcast_to(length, (slots,))])


def body(
    ngroup, ninst,
    tbl, cache, q, kv, out,
    cbuf, s1a, s1b, s1c, s1d, r1a, r1b, r1c, r1d, s2, r2,
    qx, kvx, qs, kbias, fbias, sref, mref, oo,
    ld, s1sem, r1sem, s2sem, r2sem, xs, xr, osem, orsem, lsem,
):
    g = lax.axis_index("group")
    i = lax.axis_index("inst")
    s1 = (s1a, s1b, s1c, s1d)
    r1 = (r1a, r1b, r1c, r1d)
    slots = cbuf.shape[0]
    tok = q.shape[0]
    half = lax.rem(i, 2)
    partner = i + 1 - 2 * half
    hw = q.shape[1] // 2
    kw = KVH * HD // 2

    loads = [
        pltpu.make_async_copy(cache.at[0], cbuf, ld.at[0]),
        pltpu.make_async_copy(q.at[:, pl.ds(half * hw, hw)], qx.at[0], ld.at[1]),
        pltpu.make_async_copy(kv.at[:, pl.ds(half * kw, kw)], kvx.at[0, 0], ld.at[2]),
        pltpu.make_async_copy(kv.at[:, pl.ds(2 * kw + half * kw, kw)], kvx.at[0, 1], ld.at[3]),
    ]
    for c in loads:
        c.start()

    barrier = pltpu.get_barrier_semaphore()

    def greet_group(d, _):
        pl.semaphore_signal(barrier, inc=1, device_id=(lax.rem(g + d, ngroup), i), device_id_type=MESH)
        return 0

    def greet_inst(e, _):
        pl.semaphore_signal(barrier, inc=1, device_id=(g, lax.rem(i + e, ninst)), device_id_type=MESH)
        return 0

    lax.fori_loop(1, ngroup, greet_group, 0)
    lax.fori_loop(1, ninst, greet_inst, 0)

    def tile_cols(c):
        return (c * HD, (KVH + c) * HD, (KVH // 2 + c) * HD, (KVH + KVH // 2 + c) * HD)

    def permute1(c):
        def step(p, _):
            s = tbl[p]
            for t, col in enumerate(tile_cols(c)):
                s1[c][p, t] = cbuf[s, :, col : col + HD]
            return 0

        lax.fori_loop(0, slots, step, 0, unroll=4)
        for p in range(slots // ngroup):
            r1[c][p] = s1[c][p]

    per = slots // ngroup

    def send1(c):
        def step(d, _):
            pltpu.make_async_remote_copy(
                src_ref=s1[c].at[pl.ds(per * d, per)],
                dst_ref=r1[c].at[pl.ds(per * d, per)],
                send_sem=s1sem.at[c],
                recv_sem=r1sem.at[c],
                device_id=(lax.rem(g + d, ngroup), i),
                device_id_type=MESH,
            ).start()
            return 0

        lax.fori_loop(1, ngroup, step, 0)

    def all1(c):
        return pltpu.make_async_remote_copy(
            src_ref=s1[c].at[pl.ds(per, slots - per)],
            dst_ref=r1[c].at[pl.ds(per, slots - per)],
            send_sem=s1sem.at[c],
            recv_sem=r1sem.at[c],
            device_id=(lax.rem(g + 1, ngroup), i),
            device_id_type=MESH,
        )

    items = slots // (ninst // 2)
    blk = cbuf.shape[1]

    def permute2(c):
        def gather(e, ref):
            j = lax.rem(i + e, ninst)
            w = j // 2
            h = lax.rem(j, 2)

            def step(k, _):
                idx = tbl[slots + w * items + k]
                for t in range(2):
                    ref[c, e, t, pl.ds(k * blk, blk), :] = r1[c][idx, 2 * h + t]
                return 0

            lax.fori_loop(0, items, step, 0, unroll=4)

        gather(0, r2)

        def outer(e, _):
            gather(e, s2)
            return 0

        lax.fori_loop(1, ninst, outer, 0)

    def send2(c):
        def step(e, _):
            pltpu.make_async_remote_copy(
                src_ref=s2.at[c, e],
                dst_ref=r2.at[c, e],
                send_sem=s2sem.at[c],
                recv_sem=r2sem.at[c],
                device_id=(g, lax.rem(i + e, ninst)),
                device_id_type=MESH,
            ).start()
            return 0

        lax.fori_loop(1, ninst, step, 0)

    def all2(c):
        return pltpu.make_async_remote_copy(
            src_ref=s2.at[c, pl.ds(1, ninst - 1)],
            dst_ref=r2.at[c, pl.ds(1, ninst - 1)],
            send_sem=s2sem.at[c],
            recv_sem=r2sem.at[c],
            device_id=(g, lax.rem(i + 1, ninst)),
            device_id_type=MESH,
        )

    other = 1 - half
    swaps = [
        pltpu.make_async_remote_copy(
            src_ref=src, dst_ref=dst, send_sem=xs.at[n], recv_sem=xr.at[n],
            device_id=(g, partner), device_id_type=MESH,
        )
        for n, (src, dst) in enumerate([
            (q.at[:, pl.ds(other * hw, hw)], qx.at[1]),
            (kv.at[:, pl.ds(other * kw, kw)], kvx.at[1, 0]),
            (kv.at[:, pl.ds(2 * kw + other * kw, kw)], kvx.at[1, 1]),
        ])
    ]

    loads[0].wait()
    permute1(0)
    pl.semaphore_wait(barrier, ngroup - 1 + ninst - 1)
    send1(0)
    for copy in swaps:
        copy.start()
    for c in range(1, NCH):
        permute1(c)
        send1(c)

    length = tbl[2 * slots]
    ctx = items * blk
    eye = (
        lax.broadcasted_iota(jnp.int32, (tok, tok), 0)
        == lax.broadcasted_iota(jnp.int32, (tok, tok), 1)
    )
    for b in range(qs.shape[0] // tok):
        qs[pl.ds(b * tok, tok), HD:] = jnp.where(eye, 1.0, 0.0).astype(jnp.bfloat16)
    row = lax.broadcasted_iota(jnp.int32, (ctx, HD), 0)
    for e in range(ninst):
        source = lax.rem(i - e + ninst, ninst)
        kbias[e] = jnp.where(row + source * ctx < length, 0.0, BIG).astype(jnp.bfloat16)
    key = lax.broadcasted_iota(jnp.int32, (tok, HD), 0)
    query = lax.broadcasted_iota(jnp.int32, (tok, HD), 1)
    tri = jnp.where(key <= query, 0.0, BIG).astype(jnp.bfloat16)
    flag = jnp.full((tok, HD), half, jnp.int32)
    fbias[0, :tok, :] = tri
    fbias[0, tok:, :] = jnp.where(flag == 1, 0.0, BIG).astype(jnp.bfloat16)
    fbias[1, :tok, :] = jnp.where(flag == 0, 0.0, BIG).astype(jnp.bfloat16)
    fbias[1, tok:, :] = tri

    for c in range(NCH):
        all1(c).wait_recv()
        permute2(c)
        send2(c)

    for copy in loads[1:]:
        copy.wait()
    for copy in swaps:
        copy.wait_recv()

    groups = hw // (KVH // 2 * HD)
    rows = groups * tok
    coef = float(HD) ** -0.5 * 1.4426950408889634
    nt = (((1,), (1,)), ((), ()))

    def score(qv, k, bias):
        return lax.dot_general(
            qv, jnp.concatenate([k, bias], axis=1), nt, preferred_element_type=jnp.float32
        )

    def attention(c):
        for h in range(2):
            for j in range(groups):
                qs[pl.ds((h * groups + j) * tok, tok), :HD] = qx[h, :, pl.ds((groups * c + j) * HD, HD)]
        kf = jnp.concatenate([kvx[0, 0, :, pl.ds(c * HD, HD)], kvx[1, 0, :, pl.ds(c * HD, HD)]], axis=0)
        vf = jnp.concatenate([kvx[0, 1, :, pl.ds(c * HD, HD)], kvx[1, 1, :, pl.ds(c * HD, HD)]], axis=0)
        for h in range(2):
            s = score(qs[pl.ds(h * rows, rows), :], kf, fbias[h])
            sref[ninst, pl.ds(h * rows, rows), :] = s
            mref[pl.ds(h * rows, rows), :] = jnp.maximum(s[:, :HD], s[:, HD:])

        def first(e, _):
            s = score(qs[...], r2[c, e, 0], kbias[e])
            sref[e] = s
            mref[...] = jnp.maximum(mref[...], jnp.maximum(s[:, :HD], s[:, HD:]))
            return 0

        lax.fori_loop(0, ninst, first, 0)
        rb = 2 * tok
        ones = jnp.ones((ctx, HD), jnp.bfloat16)

        def second(b, _):
            span = pl.ds(pl.multiple_of(b * rb, rb), rb)
            m = jnp.max(mref[span, :], axis=1, keepdims=True)
            total = jnp.zeros((rb, 2 * HD), jnp.float32)
            for e in range(ninst + 1):
                p = jnp.exp2((sref[e, span, :] - m) * coef).astype(jnp.bfloat16)
                v = r2[c, e, 1] if e < ninst else vf
                total = total + jnp.dot(
                    p, jnp.concatenate([v, ones], axis=1), preferred_element_type=jnp.float32
                )
            o = (total[:, :HD] / total[:, HD:]).astype(jnp.bfloat16)
            oo[c, 2 * b] = o[:tok]
            oo[c, 2 * b + 1] = o[tok:]
            return 0

        lax.fori_loop(0, qs.shape[0] // rb, second, 0)

    pending = []
    for c in range(NCH):
        all2(c).wait_recv()
        attention(c)
        for j in range(groups):
            col = half * hw + (c * groups + j) * HD
            mine = pltpu.make_async_copy(oo.at[c, j], out.at[:, pl.ds(col, HD)], lsem.at[c, j])
            mine.start()
            theirs = pltpu.make_async_remote_copy(
                src_ref=oo.at[c, groups + j],
                dst_ref=out.at[:, pl.ds(col, HD)],
                send_sem=osem.at[c, j],
                recv_sem=orsem.at[c, j],
                device_id=(g, partner),
                device_id_type=MESH,
            )
            theirs.start()
            pending.append((mine, theirs))
    for copy in swaps:
        copy.wait_send()
    for c in range(NCH):
        all1(c).wait_send()
        all2(c).wait_send()
    for mine, theirs in pending:
        mine.wait()
        theirs.wait()


def on_device(old_cache, block_table, place_after, context_len, queries, new_kv):
    ninst = lax.axis_size("inst")
    ngroup = lax.axis_size("group")
    slots, blk, width = old_cache.shape[1:]
    tok, qw = queries.shape
    per_inst = block_table.shape[1] // ninst
    tbl = tables(block_table, place_after, context_len, slots, per_inst)
    ctx = per_inst * blk
    groups = qw // (KVH * HD)
    bf = jnp.bfloat16
    piece = pltpu.VMEM((slots, 4, blk, HD), bf)
    rows = 2 * groups * tok
    dma = pltpu.SemaphoreType.DMA
    return pl.pallas_call(
        functools.partial(body, ngroup, ninst),
        out_shape=jax.ShapeDtypeStruct((tok, qw), bf),
        in_specs=[pl.BlockSpec(memory_space=pltpu.SMEM)] + [pl.BlockSpec(memory_space=pl.ANY)] * 3,
        out_specs=pl.BlockSpec(memory_space=pl.ANY),
        scratch_shapes=[
            pltpu.VMEM((slots, blk, width), bf),
            *[piece] * (2 * NCH),
            pltpu.VMEM((NCH, ninst, 2, ctx, HD), bf),
            pltpu.VMEM((NCH, ninst, 2, ctx, HD), bf),
            pltpu.VMEM((2, tok, qw // 2), bf),
            pltpu.VMEM((2, 2, tok, KVH // 2 * HD), bf),
            pltpu.VMEM((rows, 2 * HD), bf),
            pltpu.VMEM((ninst, ctx, HD), bf),
            pltpu.VMEM((2, 2 * tok, HD), bf),
            pltpu.VMEM((ninst + 1, rows, ctx), jnp.float32),
            pltpu.VMEM((rows, HD), jnp.float32),
            pltpu.VMEM((NCH, 2 * groups, tok, HD), bf),
            dma((4,)), dma((NCH,)), dma((NCH,)), dma((NCH,)), dma((NCH,)),
            dma((3,)), dma((3,)), dma((NCH, groups)), dma((NCH, groups)), dma((NCH, groups)),
        ],
        compiler_params=pltpu.CompilerParams(
            collective_id=0, has_side_effects=True, vmem_limit_bytes=60 * 1024 * 1024
        ),
    )(tbl, old_cache, queries, new_kv)


def solution(mesh):
    return jax.shard_map(
        on_device,
        mesh=mesh,
        in_specs=(
            P("inst", "group", None, None),
            P(),
            P(),
            P(),
            P(("group", "inst"), None),
            P(("group", "inst"), None),
        ),
        out_specs=P(("group", "inst"), None),
        check_vma=False,
    )
```

time: 327 us -> 146 us (0.45)
  the two profiles are of different devices: /device:TPU:6 before, /device:TPU:2 now
where the time goes in v1:
time: 146 us; the launch traced here: 144 us
  Pallas kernels  138 us (95%)
  local copies, waits for them, and re-layouts  3.19 us (2%)
  other arithmetic  2.86 us (2%)
    pallas_call x1, Pallas kernels, on_device(): pl.pallas_call(functools.partial(body, ngroup, ninst), out_shape=jax.Shap...  138 us

profile of v1, /device:TPU:2, one launch (start us, length us, event | category | flops | bytes accessed | tf_op | source)
XLA Modules:
  0.0 144.0 jit_solution(653519817707448049)
XLA Ops:
  0.0 0.0 copy-start
  0.0 1.3 broadcast_multiply_fusion
  1.4 0.6 broadcast_in_dim.55
  2.0 0.1 iota_add_fusion
  2.1 0.1 add.79
  2.2 0.0 copy-done
  2.2 0.1 constant_dynamic-slice_fusion
  2.3 0.1 eq.31
  2.3 0.3 select_reduce_fusion.1
  2.6 0.2 convert_reduce_fusion.1
  2.8 0.1 select_reduce_fusion.2
  3.0 0.2 convert_reduce_fusion
  3.2 0.6 pad_add_fusion.tbl
  3.8 137.9 %shard_map.64 = bf16[128,4096]{1,0:T(8,128)(2,1)} custom-call(s32[192]{0:T(256)} %pad_add_fusion.tbl, bf16[1,64,16,2048]{3,2,1,0:T(8,128)(2,1)} %cache.1, bf16[128,4096]{1,0:T(8,128)(2,1)} %q.1, bf16[128,2048]{1,0:T(8,128)(2,1)} %kv.1), custom_call_target="tpu_custom_call" | custom-call | tf_op jit(solution)/shard_map/pallas_call | solution.py:314
  141.7 2.3 %copy.8 = bf16[128,4096]{1,0:T(8,128)(2,1)} copy(bf16[128,4096]{1,0:T(8,128)(2,1)} %shard_map.64) | data formatting | bytes 2097152
  (4 shorter events, 0.1 us)
Async XLA Ops:
  0.0 2.2 %copy-start = (s32[128,128]{1,0:T(8,128)S(1)}, s32[128,128]{1,0:T(8,128)}, u32[]{:S(2)}) copy-start(s32[128,128]{1,0:T(8,128)} %param.7) | copy-start | bytes 196612

commit v2 on v1

v2 whole, which is shorter than its diff:
```python
import functools

import jax
import jax.numpy as jnp
from jax import lax
from jax.experimental import pallas as pl
from jax.experimental.pallas import tpu as pltpu
from jax.sharding import PartitionSpec as P

KVH = 8
HD = 128
NCH = KVH
LAG = 3
BIG = -1e30
COEF = float(HD) ** -0.5 * 1.4426950408889634
MESH = pl.DeviceIdType.MESH


def tables(block_table, place_after, context_len, slots, per_inst):
    g = lax.axis_index("group")
    i = lax.axis_index("inst")
    ngroup = lax.axis_size("group")
    rgroup = slots // per_inst
    columns = lax.dynamic_slice_in_dim(block_table, i * per_inst, per_inst, 1)
    kk = lax.broadcasted_iota(jnp.int32, columns.shape, 1)
    keys = (place_after[:, None] * per_inst + kk).reshape(1, -1)
    places = columns.reshape(1, -1)
    ids = jnp.arange(slots, dtype=jnp.int32)
    mine = g * slots + ids
    key_of_slot = jnp.sum(jnp.where(places == mine[:, None], keys, 0), axis=1)
    rank = jnp.sum((key_of_slot[None, :] < key_of_slot[:, None]).astype(jnp.int32), axis=1)
    pos = (rank - g * (slots // ngroup) + slots) % slots
    send = jnp.sum(jnp.where(pos[None, :] == ids[:, None], ids[None, :], 0), axis=1)
    place_of_item = jnp.sum(jnp.where(keys == mine[:, None], places, 0), axis=1)
    owner = place_of_item // slots
    same = (owner[None, :] == owner[:, None]) & (ids[None, :] < ids[:, None])
    second = jnp.sum(same.astype(jnp.int32), axis=1)
    recv = ((g - owner + ngroup) % ngroup) * (slots // ngroup) + second
    slot = g * rgroup + i // 2
    length = jnp.sum(jnp.where(place_after == slot, context_len, 0))
    return jnp.concatenate([send, recv, jnp.broadcast_to(length, (slots,))])


def body(ngroup, ninst, tbl, cache, q, kv, out, *scratch):
    s1, r1 = scratch[:NCH], scratch[NCH : 2 * NCH]
    (cbuf, s2, r2, qx, kvx, qs, kbias, fbias, sref, sfresh, mref, own, stat, oo, orecv, st, strecv,
     ostage, ld, s1sem, r1sem, s2sem, r2sem, xs, xr, osem, orsem, tsem, trsem, lsem) = scratch[2 * NCH :]
    g = lax.axis_index("group")
    i = lax.axis_index("inst")
    slots, blk = cbuf.shape[:2]
    tok = q.shape[0]
    half = lax.rem(i, 2)
    sgn = 1 - 2 * half
    partner = i + sgn
    kw = KVH * HD
    groups = q.shape[1] // kw
    rows = groups * tok
    per = slots // ngroup
    items = slots // (ninst // 2)
    ctx = items * blk
    sides = ninst // 2

    loads = [
        pltpu.make_async_copy(cache.at[0], cbuf, ld.at[0]),
        pltpu.make_async_copy(q, qx.at[0], ld.at[1]),
        pltpu.make_async_copy(kv, kvx, ld.at[2]),
    ]
    for copy in loads:
        copy.start()

    barrier = pltpu.get_barrier_semaphore()

    def greet_group(d, _):
        pl.semaphore_signal(barrier, inc=1, device_id=(lax.rem(g + d, ngroup), i), device_id_type=MESH)
        return 0

    def greet_inst(e, _):
        pl.semaphore_signal(barrier, inc=1, device_id=(g, lax.rem(i + e, ninst)), device_id_type=MESH)
        return 0

    lax.fori_loop(1, ngroup, greet_group, 0)
    lax.fori_loop(1, ninst, greet_inst, 0)

    def permute1(c):
        def step(p, _):
            s = tbl[p]
            s1[c][p, 0] = cbuf[s, :, c * HD : (c + 1) * HD]
            s1[c][p, 1] = cbuf[s, :, kw + c * HD : kw + (c + 1) * HD]
            return 0

        lax.fori_loop(0, slots, step, 0, unroll=8)
        for p in range(per):
            r1[c][p] = s1[c][p]

    def send1(c):
        def step(d, _):
            pltpu.make_async_remote_copy(
                src_ref=s1[c].at[pl.ds(per * d, per)],
                dst_ref=r1[c].at[pl.ds(per * d, per)],
                send_sem=s1sem.at[c],
                recv_sem=r1sem.at[c],
                device_id=(lax.rem(g + d, ngroup), i),
                device_id_type=MESH,
            ).start()
            return 0

        lax.fori_loop(1, ngroup, step, 0)

    def all1(c):
        return pltpu.make_async_remote_copy(
            src_ref=s1[c].at[pl.ds(per, slots - per)],
            dst_ref=r1[c].at[pl.ds(per, slots - per)],
            send_sem=s1sem.at[c],
            recv_sem=r1sem.at[c],
            device_id=(lax.rem(g + 1, ngroup), i),
            device_id_type=MESH,
        )

    def target(n):
        step = (0, -1, 2, -3)[n]
        return lax.rem(i + sgn * step + ninst, ninst)

    def permute2(c):
        for n in range(sides):
            base = slots + target(n) // 2 * items

            def step(k, _):
                idx = tbl[base + k]
                for t in range(2):
                    if n == 0:
                        r2[c, 0, t, pl.ds(k * blk, blk), :] = r1[c][idx, t]
                    else:
                        s2[c, n - 1, t, pl.ds(k * blk, blk), :] = r1[c][idx, t]
                return 0

            lax.fori_loop(0, items, step, 0, unroll=8)

    def send2(c):
        for n in range(sides - 1, 0, -1):
            pltpu.make_async_remote_copy(
                src_ref=s2.at[c, n - 1],
                dst_ref=r2.at[c, n],
                send_sem=s2sem.at[c],
                recv_sem=r2sem.at[c],
                device_id=(g, target(n)),
                device_id_type=MESH,
            ).start()

    def all2(c):
        return pltpu.make_async_remote_copy(
            src_ref=s2.at[c],
            dst_ref=r2.at[c, pl.ds(1, sides - 1)],
            send_sem=s2sem.at[c],
            recv_sem=r2sem.at[c],
            device_id=(g, partner),
            device_id_type=MESH,
        )

    def to_partner(src, dst, ssem, rsem):
        return pltpu.make_async_remote_copy(
            src_ref=src, dst_ref=dst, send_sem=ssem, recv_sem=rsem,
            device_id=(g, partner), device_id_type=MESH,
        )

    swap = to_partner(q, qx.at[1], xs, xr)

    loads[0].wait()
    permute1(0)
    pl.semaphore_wait(barrier, ngroup - 1 + ninst - 1)
    send1(0)
    swap.start()
    for c in range(1, NCH):
        permute1(c)
        send1(c)

    length = tbl[2 * slots]
    eye = (
        lax.broadcasted_iota(jnp.int32, (tok, tok), 0)
        == lax.broadcasted_iota(jnp.int32, (tok, tok), 1)
    )
    for b in range(groups):
        qs[pl.ds(b * tok, tok), HD:] = jnp.where(eye, 1.0, 0.0).astype(jnp.bfloat16)
    row = lax.broadcasted_iota(jnp.int32, (ctx, HD), 0)
    for n in range(sides):
        source = lax.rem(i - sgn * n + ninst, ninst)
        kbias[n] = jnp.where(row + source * ctx < length, 0.0, BIG).astype(jnp.bfloat16)
    key = lax.broadcasted_iota(jnp.int32, (tok, HD), 0)
    query = lax.broadcasted_iota(jnp.int32, (tok, HD), 1)
    fbias[0] = jnp.where(key <= query, 0.0, BIG).astype(jnp.bfloat16)
    flag = jnp.full((tok, HD), half, jnp.int32)
    fbias[1] = jnp.where(flag == 0, 0.0, BIG).astype(jnp.bfloat16)

    nt = (((1,), (1,)), ((), ()))

    def score(k, bias):
        return lax.dot_general(
            qs[...], jnp.concatenate([k, bias], axis=1), nt, preferred_element_type=jnp.float32
        )

    lane = lax.broadcasted_iota(jnp.int32, (tok, HD), 1)
    rb = 2 * tok
    ones = jnp.ones((ctx, HD), jnp.bfloat16)

    def attend(c, h):
        for j in range(groups):
            qs[pl.ds(j * tok, tok), :HD] = qx[h, :, (groups * c + j) * HD : (groups * c + j + 1) * HD]
        s = score(kvx[:, c * HD : (c + 1) * HD], fbias[h])
        sfresh[...] = s
        mref[...] = s

        def first(n, _):
            s = score(r2[c, n, 0], kbias[n])
            sref[n] = s
            mref[...] = jnp.maximum(mref[...], jnp.maximum(s[:, :HD], s[:, HD:]))
            return 0

        lax.fori_loop(0, sides, first, 0)
        vf = kvx[:, kw + c * HD : kw + (c + 1) * HD]
        stats = jnp.zeros((tok, HD), jnp.float32)
        for b in range(rows // rb):
            span = pl.ds(b * rb, rb)
            m = jnp.max(mref[span, :], axis=1, keepdims=True)
            total = jnp.dot(
                jnp.exp2((sfresh[span, :] - m) * COEF).astype(jnp.bfloat16),
                jnp.concatenate([vf, ones[:tok]], axis=1),
                preferred_element_type=jnp.float32,
            )
            for n in range(sides):
                p = jnp.exp2((sref[n, span, :] - m) * COEF).astype(jnp.bfloat16)
                total = total + jnp.dot(
                    p, jnp.concatenate([r2[c, n, 1], ones], axis=1), preferred_element_type=jnp.float32
                )
            o = total[:, :HD] / total[:, HD:]
            for j in range(rb // tok):
                at = b * (rb // tok) + j
                part = slice(j * tok, (j + 1) * tok)
                stats = jnp.where(lane == at, m[part], stats)
                stats = jnp.where(lane == groups + at, total[part, HD:], stats)
                if h == 0:
                    own[c % 2, at] = o[part]
                else:
                    oo[c, at] = o[part].astype(jnp.bfloat16)
        if h == 0:
            stat[c % 2] = stats
        else:
            st[c] = jnp.transpose(stats)[: 2 * groups]

    def combine(c):
        oparts[c].wait_recv()
        tparts[c].wait_recv()
        fill = jnp.zeros((tok - 2 * groups, HD), jnp.float32)
        theirs = jnp.transpose(jnp.concatenate([strecv[c], fill], axis=0))
        mine = stat[c % 2]
        top = jnp.maximum(mine, theirs)
        for j in range(groups):
            a, b = slice(j, j + 1), slice(groups + j, groups + j + 1)
            wa = mine[:, b] * jnp.exp2((mine[:, a] - top[:, a]) * COEF)
            wb = theirs[:, b] * jnp.exp2((theirs[:, a] - top[:, a]) * COEF)
            r = 1.0 / (wa + wb)
            o = own[c % 2, j] * (wa * r) + orecv[c, j].astype(jnp.float32) * (wb * r)
            ostage[c, :, j * HD : (j + 1) * HD] = o.astype(jnp.bfloat16)
        outs[c].start()

    oparts = [to_partner(oo.at[c], orecv.at[c], osem.at[c], orsem.at[c]) for c in range(NCH)]
    tparts = [to_partner(st.at[c], strecv.at[c], tsem.at[c], trsem.at[c]) for c in range(NCH)]
    outs = [
        pltpu.make_async_copy(
            ostage.at[c], out.at[:, pl.ds(c * groups * HD, groups * HD)], lsem.at[c]
        )
        for c in range(NCH)
    ]

    def attention(c):
        if c == 0:
            for copy in loads[1:]:
                copy.wait()
            swap.wait_recv()
        all2(c).wait_recv()
        attend(c, 1)
        tparts[c].start()
        oparts[c].start()
        attend(c, 0)
        if c:
            combine(c - 1)

    for c in range(NCH):
        all1(c).wait_recv()
        permute2(c)
        send2(c)
        if c >= LAG:
            attention(c - LAG)
    for c in range(NCH - LAG, NCH):
        attention(c)
    combine(NCH - 1)
    swap.wait_send()
    for c in range(NCH):
        all1(c).wait_send()
        all2(c).wait_send()
        oparts[c].wait_send()
        tparts[c].wait_send()
        outs[c].wait()


def on_device(old_cache, block_table, place_after, context_len, queries, new_kv):
    ninst = lax.axis_size("inst")
    ngroup = lax.axis_size("group")
    slots, blk, width = old_cache.shape[1:]
    tok, qw = queries.shape
    per_inst = block_table.shape[1] // ninst
    tbl = tables(block_table, place_after, context_len, slots, per_inst)
    ctx = per_inst * blk
    groups = qw // (KVH * HD)
    rows = groups * tok
    sides = ninst // 2
    bf, f32 = jnp.bfloat16, jnp.float32
    dma = pltpu.SemaphoreType.DMA
    return pl.pallas_call(
        functools.partial(body, ngroup, ninst),
        out_shape=jax.ShapeDtypeStruct((tok, qw), bf),
        in_specs=[pl.BlockSpec(memory_space=pltpu.SMEM)] + [pl.BlockSpec(memory_space=pl.ANY)] * 3,
        out_specs=pl.BlockSpec(memory_space=pl.ANY),
        scratch_shapes=[
            *[pltpu.VMEM((slots, 2, blk, HD), bf)] * (2 * NCH),
            pltpu.VMEM((slots, blk, width), bf),
            pltpu.VMEM((NCH, sides - 1, 2, ctx, HD), bf),
            pltpu.VMEM((NCH, sides, 2, ctx, HD), bf),
            pltpu.VMEM((2, tok, qw), bf),
            pltpu.VMEM((tok, 2 * KVH * HD), bf),
            pltpu.VMEM((rows, 2 * HD), bf),
            pltpu.VMEM((sides, ctx, HD), bf),
            pltpu.VMEM((2, tok, HD), bf),
            pltpu.VMEM((sides, rows, ctx), f32),
            pltpu.VMEM((rows, tok), f32),
            pltpu.VMEM((rows, HD), f32),
            pltpu.VMEM((2, groups, tok, HD), f32),
            pltpu.VMEM((2, tok, HD), f32),
            pltpu.VMEM((NCH, groups, tok, HD), bf),
            pltpu.VMEM((NCH, groups, tok, HD), bf),
            pltpu.VMEM((NCH, 2 * groups, HD), f32),
            pltpu.VMEM((NCH, 2 * groups, HD), f32),
            pltpu.VMEM((NCH, tok, groups * HD), bf),
            dma((3,)), dma((NCH,)), dma((NCH,)), dma((NCH,)), dma((NCH,)), dma, dma,
            dma((NCH,)), dma((NCH,)), dma((NCH,)), dma((NCH,)), dma((NCH,)),
        ],
        compiler_params=pltpu.CompilerParams(
            collective_id=0, has_side_effects=True, vmem_limit_bytes=60 * 1024 * 1024
        ),
    )(tbl, old_cache, queries, new_kv)


def solution(mesh):
    return jax.shard_map(
        on_device,
        mesh=mesh,
        in_specs=(
            P("inst", "group", None, None),
            P(),
            P(),
            P(),
            P(("group", "inst"), None),
            P(("group", "inst"), None),
        ),
        out_specs=P(("group", "inst"), None),
        check_vma=False,
    )
```

time: 146 us -> 129 us (0.88)
  Pallas kernels: 138 us -> 121 us
    pallas_call x1, Pallas kernels: 138 us -> 121 us  [on_device(): pl.pallas_call(functools.partial(body, ngroup, ninst), out_shape=jax.Shap...]
where the time goes in v2:
time: 129 us; the launch traced here: 127 us
  Pallas kernels  121 us (94%)
  local copies, waits for them, and re-layouts  3.19 us (2%)
  other arithmetic  2.86 us (2%)
    pallas_call x1, Pallas kernels, on_device(): pl.pallas_call(functools.partial(body, ngroup, ninst), out_shape=jax.Shap...  121 us

profile of v2, /device:TPU:2, one launch (start us, length us, event | category | flops | bytes accessed | tf_op | source)
XLA Modules:
  0.0 127.2 jit_solution(7604788899547541711)
XLA Ops:
  0.0 0.0 copy-start
  0.0 1.3 %broadcast_multiply_fusion = (s32[128]{0:T(128)S(1)}, s32[]{:T(128)}) fusion(s32[128]{0:T(128)} %param.8, s32[128]{0:T(128)} %param.9, s32[]{:T(128)S(6)} %add.87), kind=kLoop, calls=%fused_computation.27 | loop fusion | flops 511 | bytes 1544 | tf_op jit(solution)/shard_map/mul | solution.py:26
  1.4 0.6 broadcast_in_dim.55
  2.0 0.1 iota_add_fusion
  2.1 0.1 add.79
  2.2 0.0 copy-done
  2.2 0.1 constant_dynamic-slice_fusion
  2.3 0.1 eq.31
  2.3 0.3 select_reduce_fusion.1
  2.6 0.2 convert_reduce_fusion.1
  2.8 0.1 select_reduce_fusion.2
  3.0 0.2 convert_reduce_fusion
  3.2 0.6 pad_add_fusion.tbl
  3.8 121.1 %shard_map.64 = bf16[128,4096]{1,0:T(8,128)(2,1)} custom-call(s32[192]{0:T(256)} %pad_add_fusion.tbl, bf16[1,64,16,2048]{3,2,1,0:T(8,128)(2,1)} %cache.1, bf16[128,4096]{1,0:T(8,128)(2,1)} %q.1, bf16[128,2048]{1,0:T(8,128)(2,1)} %kv.1), custom_call_target="tpu_custom_call" | custom-call | tf_op jit(solution)/shard_map/pallas_call | solution.py:317
  124.9 2.3 %copy.8 = bf16[128,4096]{1,0:T(8,128)(2,1)} copy(bf16[128,4096]{1,0:T(8,128)(2,1)} %shard_map.64) | data formatting | bytes 2097152
  (4 shorter events, 0.1 us)
Async XLA Ops:
  0.0 2.2 %copy-start = (s32[128,128]{1,0:T(8,128)S(1)}, s32[128,128]{1,0:T(8,128)}, u32[]{:S(2)}) copy-start(s32[128,128]{1,0:T(8,128)} %param.7) | copy-start | bytes 196612

commit v3 on v2

v3 whole, which is shorter than its diff:
```python
import functools

import jax
import jax.numpy as jnp
from jax import lax
from jax.experimental import pallas as pl
from jax.experimental.pallas import tpu as pltpu
from jax.sharding import PartitionSpec as P

KVH = 8
HD = 128
PARTS = [(0, (0,)), (0, (1,))] + [(c, (0, 1)) for c in range(1, KVH)]
EARLY = 4
VLIM = 46
BIG = -1e30
COEF = float(HD) ** -0.5 * 1.4426950408889634
MESH = pl.DeviceIdType.MESH


def onehot(cond):
    return jnp.where(cond, 1.0, 0.0).astype(jnp.bfloat16)


def tables(blocks, places, tab, g, i, ngroup, slots, items):
    reqs, nblk = blocks.shape
    rgroup = slots // items
    value = blocks[...]
    owner = (value // slots).astype(jnp.float32).astype(jnp.bfloat16)
    local = (value % slots).astype(jnp.float32).astype(jnp.bfloat16)
    k = lax.broadcasted_iota(jnp.int32, (nblk, HD), 0)
    lane = lax.broadcasted_iota(jnp.int32, (nblk, HD), 1)
    pick = onehot(k == i * items + lane % items)
    row = lax.broadcasted_iota(jnp.int32, (rgroup * ngroup, reqs), 0)
    place = row % ngroup * rgroup + row // ngroup
    order = onehot(jnp.broadcast_to(places[...], (rgroup * ngroup, reqs)) == place)

    def by_group(array):
        columns = jnp.dot(array, pick, preferred_element_type=jnp.float32).astype(jnp.bfloat16)
        rows = jnp.dot(order, columns, preferred_element_type=jnp.float32)
        within = lax.broadcasted_iota(jnp.int32, (ngroup, HD), 1) // items
        result = rows[:ngroup]
        for w in range(1, rgroup):
            result = jnp.where(within == w, rows[w * ngroup : (w + 1) * ngroup], result)
        return result.astype(jnp.int32)

    owners, locals_ = by_group(owner), by_group(local)
    item = lax.broadcasted_iota(jnp.int32, (ngroup, HD), 1)
    hit = (owners == g) & (item < slots)
    first = jnp.min(jnp.where(hit, item, HD), axis=1, keepdims=True)
    last = jnp.max(jnp.where(hit, item, -1), axis=1, keepdims=True)
    one = jnp.sum(jnp.where(item == first, locals_, 0), axis=1, keepdims=True)
    two = jnp.sum(jnp.where(item == last, locals_, 0), axis=1, keepdims=True)
    tab[:ngroup, :] = jnp.where(item == 0, one, two)
    mine = jnp.sum(
        jnp.where(lax.broadcasted_iota(jnp.int32, (ngroup, HD), 0) == g, owners, 0), axis=0, keepdims=True
    )
    across = jnp.broadcast_to(mine, (HD, HD)).astype(jnp.float32)
    down = jnp.transpose(across)
    t0 = lax.broadcasted_iota(jnp.int32, (HD, HD), 0)
    t1 = lax.broadcasted_iota(jnp.int32, (HD, HD), 1)
    before = jnp.sum(jnp.where((across == down) & (t0 < t1), 1, 0), axis=0, keepdims=True)
    per = slots // ngroup
    arrival = (g - mine + ngroup) % ngroup * per + jnp.minimum(before, per - 1)
    tab[ngroup:, :] = jnp.broadcast_to(arrival, (tab.shape[0] - ngroup, HD))


def body(ngroup, ninst, blocks_hbm, places_hbm, lengths_hbm, cache_hbm, q, kv, out, *scratch):
    parts = len(PARTS)
    s1, r1 = scratch[:parts], scratch[parts : 2 * parts]
    (cache, blocks, places, lengths, tab, tbl, s2, r2, qx, kvx, qs, kbias, fbias, sref, sfresh, mref, own, stat, oo, orecv, st, strecv,
     ld, s1sem, r1sem, s2sem, r2sem, xs, xr, osem, orsem, tsem, trsem) = scratch[2 * parts :]
    g = lax.axis_index("group")
    i = lax.axis_index("inst")
    slots, blk = cache.shape[:2]
    tok = q.shape[0]
    half = lax.rem(i, 2)
    sgn = 1 - 2 * half
    partner = i + sgn
    kw = KVH * HD
    groups = q.shape[1] // kw
    qw = groups * HD
    rows = groups * tok
    per = slots // ngroup
    items = slots // (ninst // 2)
    ctx = items * blk
    sides = ninst // 2

    pairs = [
        (blocks_hbm, blocks), (places_hbm, places), (lengths_hbm, lengths),
        (cache_hbm.at[0], cache), (kv, kvx), (q, qx.at[1]),
    ]
    loads = [pltpu.make_async_copy(src, dst, ld.at[n]) for n, (src, dst) in enumerate(pairs)]
    for copy in loads:
        copy.start()

    barrier = pltpu.get_barrier_semaphore()

    def greet_group(d, _):
        pl.semaphore_signal(barrier, inc=1, device_id=(lax.rem(g + d, ngroup), i), device_id_type=MESH)
        return 0

    def greet_inst(e, _):
        pl.semaphore_signal(barrier, inc=1, device_id=(g, lax.rem(i + e, ninst)), device_id_type=MESH)
        return 0

    lax.fori_loop(1, ngroup, greet_group, 0)
    lax.fori_loop(1, ninst, greet_inst, 0)


    def permute1(p):
        c, kinds = PARTS[p]

        def step(k, _):
            s = tbl[lax.rem(g + k // per, ngroup), lax.rem(k, per)]
            for n, t in enumerate(kinds):
                s1[p][k, n] = cache[s, :, t * kw + c * HD : t * kw + (c + 1) * HD]
            return 0

        lax.fori_loop(0, slots, step, 0, unroll=8)
        for k in range(per):
            r1[p][k] = s1[p][k]

    def send1(p):
        def step(d, _):
            pltpu.make_async_remote_copy(
                src_ref=s1[p].at[pl.ds(per * d, per)],
                dst_ref=r1[p].at[pl.ds(per * d, per)],
                send_sem=s1sem.at[p],
                recv_sem=r1sem.at[p],
                device_id=(lax.rem(g + d, ngroup), i),
                device_id_type=MESH,
            ).start()
            return 0

        lax.fori_loop(1, ngroup, step, 0)

    def all1(p):
        return pltpu.make_async_remote_copy(
            src_ref=s1[p].at[pl.ds(per, slots - per)],
            dst_ref=r1[p].at[pl.ds(per, slots - per)],
            send_sem=s1sem.at[p],
            recv_sem=r1sem.at[p],
            device_id=(lax.rem(g + 1, ngroup), i),
            device_id_type=MESH,
        )

    def target(n):
        step = (0, -1, 2, -3)[n]
        return lax.rem(i + sgn * step + ninst, ninst)

    def permute2(p):
        c, kinds = PARTS[p]
        for n in range(sides):
            base = target(n) // 2 * items

            def step(k, _):
                idx = tbl[ngroup, base + k]
                for m, t in enumerate(kinds):
                    if n == 0:
                        r2[c, t, 0, pl.ds(k * blk, blk), :] = r1[p][idx, m]
                    else:
                        s2[c, t, n - 1, pl.ds(k * blk, blk), :] = r1[p][idx, m]
                return 0

            lax.fori_loop(0, items, step, 0, unroll=8)

    def send2(c, t):
        for n in range(sides - 1, 0, -1):
            pltpu.make_async_remote_copy(
                src_ref=s2.at[c, t, n - 1],
                dst_ref=r2.at[c, t, n],
                send_sem=s2sem.at[c, t],
                recv_sem=r2sem.at[c, t],
                device_id=(g, target(n)),
                device_id_type=MESH,
            ).start()

    def all2(c, t):
        return pltpu.make_async_remote_copy(
            src_ref=s2.at[c, t],
            dst_ref=r2.at[c, t, pl.ds(1, sides - 1)],
            send_sem=s2sem.at[c, t],
            recv_sem=r2sem.at[c, t],
            device_id=(g, partner),
            device_id_type=MESH,
        )

    def to_partner(src, dst, ssem, rsem):
        return pltpu.make_async_remote_copy(
            src_ref=src, dst_ref=dst, send_sem=ssem, recv_sem=rsem,
            device_id=(g, partner), device_id_type=MESH,
        )

    def swap(c):
        cols = pl.ds(pl.multiple_of(c * qw, qw), qw)
        return to_partner(q.at[:, cols], qx.at[0, :, cols], xs.at[c], xr.at[c])

    for copy in loads[:3]:
        copy.wait()
    tables(blocks, places, tab, g, i, ngroup, slots, items)
    to_scalars = pltpu.make_async_copy(tab, tbl, ld.at[len(pairs)])
    to_scalars.start()
    loads[3].wait()
    to_scalars.wait()
    permute1(0)
    pl.semaphore_wait(barrier, ngroup - 1 + ninst - 1)
    send1(0)
    permute1(1)
    send1(1)
    for c in range(EARLY):
        swap(c).start()
    for p in range(2, parts):
        permute1(p)
        send1(p)

    slot = g * (slots // items) + i // 2
    length = jnp.sum(jnp.where(places[...] == slot, lengths[...], 0), axis=1, keepdims=True)
    eye = (
        lax.broadcasted_iota(jnp.int32, (tok, tok), 0)
        == lax.broadcasted_iota(jnp.int32, (tok, tok), 1)
    )
    for b in range(2 * groups):
        qs[pl.ds(b * tok, tok), HD:] = jnp.where(eye, 1.0, 0.0).astype(jnp.bfloat16)
    row = lax.broadcasted_iota(jnp.int32, (ctx, HD), 0)
    for n in range(sides):
        source = lax.rem(i - sgn * n + ninst, ninst)
        kbias[n] = jnp.where(row + source * ctx < length, 0.0, BIG).astype(jnp.bfloat16)
    key = lax.broadcasted_iota(jnp.int32, (tok, HD), 0)
    query = lax.broadcasted_iota(jnp.int32, (tok, HD), 1)
    flag = jnp.full((tok, HD), half, jnp.int32)
    fbias[0] = jnp.where(flag == 0, 0.0, BIG).astype(jnp.bfloat16)
    fbias[1] = jnp.where(key <= query, 0.0, BIG).astype(jnp.bfloat16)

    for p, (c, kinds) in enumerate(PARTS):
        all1(p).wait_recv()
        permute2(p)
        for t in kinds:
            send2(c, t)
        if 1 in kinds and c + EARLY < KVH:
            swap(c + EARLY).start()

    for copy in loads[4:]:
        copy.wait()

    nt = (((1,), (1,)), ((), ()))

    def score(qv, k, bias):
        return lax.dot_general(
            qv, jnp.concatenate([k, bias], axis=1), nt, preferred_element_type=jnp.float32
        )

    lane = lax.broadcasted_iota(jnp.int32, (tok, HD), 1)
    rb = 2 * tok
    ones = jnp.ones((ctx, HD), jnp.bfloat16)

    def scores(c):
        for h in range(2):
            for j in range(groups):
                qs[pl.ds((h * groups + j) * tok, tok), :HD] = qx[
                    h, :, pl.ds(pl.multiple_of(c * qw + j * HD, HD), HD)
                ]
            span = pl.ds(h * rows, rows)
            s = score(qs[span, :], kvx[:, pl.ds(pl.multiple_of(c * HD, HD), HD)], fbias[h])
            sfresh[span, :] = s
            mref[span, :] = s

        def first(n, _):
            s = score(qs[...], r2[c, 0, n], kbias[n])
            sref[n] = s
            mref[...] = jnp.maximum(mref[...], jnp.maximum(s[:, :HD], s[:, HD:]))
            return 0

        lax.fori_loop(0, sides, first, 0)

    def values(c, h):
        vf = kvx[:, pl.ds(pl.multiple_of(kw + c * HD, HD), HD)]
        stats = jnp.zeros((tok, HD), jnp.float32)
        for b in range(rows // rb):
            span = pl.ds(h * rows + b * rb, rb)
            m = jnp.max(mref[span, :], axis=1, keepdims=True)
            total = jnp.dot(
                jnp.exp2((sfresh[span, :] - m) * COEF).astype(jnp.bfloat16),
                jnp.concatenate([vf, ones[:tok]], axis=1),
                preferred_element_type=jnp.float32,
            )
            for n in range(sides):
                w = jnp.exp2((sref[n, span, :] - m) * COEF).astype(jnp.bfloat16)
                total = total + jnp.dot(
                    w, jnp.concatenate([r2[c, 1, n], ones], axis=1), preferred_element_type=jnp.float32
                )
            o = total[:, :HD] / total[:, HD:]
            for j in range(rb // tok):
                at = b * (rb // tok) + j
                part = slice(j * tok, (j + 1) * tok)
                stats = jnp.where(lane == at, m[part], stats)
                stats = jnp.where(lane == groups + at, total[part, HD:], stats)
                if h == 1:
                    own[lax.rem(c, 2), at] = o[part]
                else:
                    oo[c, at] = o[part].astype(jnp.bfloat16)
        if h == 1:
            stat[lax.rem(c, 2)] = stats
        else:
            st[c] = jnp.transpose(stats)[: 2 * groups]

    def opart(c):
        return to_partner(oo.at[c], orecv.at[c], osem.at[c], orsem.at[c])

    def tpart(c):
        return to_partner(st.at[c], strecv.at[c], tsem.at[c], trsem.at[c])

    def combine(c):
        opart(c).wait_recv()
        tpart(c).wait_recv()
        fill = jnp.zeros((tok - 2 * groups, HD), jnp.float32)
        theirs = jnp.transpose(jnp.concatenate([strecv[c], fill], axis=0))
        mine = stat[lax.rem(c, 2)]
        top = jnp.maximum(mine, theirs)
        for j in range(groups):
            a, b = slice(j, j + 1), slice(groups + j, groups + j + 1)
            wa = mine[:, b] * jnp.exp2((mine[:, a] - top[:, a]) * COEF)
            wb = theirs[:, b] * jnp.exp2((theirs[:, a] - top[:, a]) * COEF)
            r = 1.0 / (wa + wb)
            o = own[lax.rem(c, 2), j] * (wa * r) + orecv[c, j].astype(jnp.float32) * (wb * r)
            out[:, pl.ds(pl.multiple_of(c * qw + j * HD, HD), HD)] = o.astype(jnp.bfloat16)

    def attention(c, _):
        swap(c).wait_recv()
        all2(c, 0).wait_recv()
        scores(c)
        all2(c, 1).wait_recv()
        values(c, 0)
        tpart(c).start()
        opart(c).start()
        values(c, 1)

        @pl.when(c > 0)
        def _():
            combine(c - 1)

        return 0

    lax.fori_loop(0, KVH, attention, 0)
    combine(KVH - 1)
    for p in range(parts):
        all1(p).wait_send()

    def finish(c, _):
        swap(c).wait_send()
        all2(c, 0).wait_send()
        all2(c, 1).wait_send()
        opart(c).wait_send()
        tpart(c).wait_send()
        return 0

    lax.fori_loop(0, KVH, finish, 0)


def on_device(old_cache, block_table, place_after, context_len, queries, new_kv):
    ninst = lax.axis_size("inst")
    ngroup = lax.axis_size("group")
    slots, blk, width = old_cache.shape[1:]
    tok, qw = queries.shape
    per_inst = block_table.shape[1] // ninst
    reqs, nblk = block_table.shape
    ctx = per_inst * blk
    groups = qw // (KVH * HD)
    rows = groups * tok
    sides = ninst // 2
    bf, f32 = jnp.bfloat16, jnp.float32
    dma = pltpu.SemaphoreType.DMA
    return pl.pallas_call(
        functools.partial(body, ngroup, ninst),
        out_shape=jax.ShapeDtypeStruct((tok, qw), bf),
        in_specs=[pl.BlockSpec(memory_space=pl.ANY)] * 6,
        out_specs=pl.BlockSpec(memory_space=pltpu.VMEM),
        scratch_shapes=[
            *[pltpu.VMEM((slots, len(kinds), blk, HD), bf) for _, kinds in PARTS * 2],
            pltpu.VMEM((slots, blk, width), bf),
            pltpu.VMEM((reqs, nblk), jnp.int32),
            pltpu.VMEM((1, reqs), jnp.int32),
            pltpu.VMEM((1, reqs), jnp.int32),
            pltpu.VMEM((ngroup + 8, HD), jnp.int32),
            pltpu.SMEM((ngroup + 8, HD), jnp.int32),
            pltpu.VMEM((KVH, 2, sides - 1, ctx, HD), bf),
            pltpu.VMEM((KVH, 2, sides, ctx, HD), bf),
            pltpu.VMEM((2, tok, qw), bf),
            pltpu.VMEM((tok, 2 * KVH * HD), bf),
            pltpu.VMEM((2 * rows, 2 * HD), bf),
            pltpu.VMEM((sides, ctx, HD), bf),
            pltpu.VMEM((2, tok, HD), bf),
            pltpu.VMEM((sides, 2 * rows, ctx), f32),
            pltpu.VMEM((2 * rows, tok), f32),
            pltpu.VMEM((2 * rows, HD), f32),
            pltpu.VMEM((2, groups, tok, HD), f32),
            pltpu.VMEM((2, tok, HD), f32),
            pltpu.VMEM((KVH, groups, tok, HD), bf),
            pltpu.VMEM((KVH, groups, tok, HD), bf),
            pltpu.VMEM((KVH, 2 * groups, HD), f32),
            pltpu.VMEM((KVH, 2 * groups, HD), f32),
            dma((7,)), dma((len(PARTS),)), dma((len(PARTS),)), dma((KVH, 2)), dma((KVH, 2)),
            dma((KVH,)), dma((KVH,)), dma((KVH,)), dma((KVH,)), dma((KVH,)), dma((KVH,)),
        ],
        compiler_params=pltpu.CompilerParams(
            collective_id=0, has_side_effects=True, vmem_limit_bytes=VLIM * 1024 * 1024
        ),
    )(*(
        pltpu.with_memory_space_constraint(x, pltpu.HBM)
        for x in (block_table, place_after[None], context_len[None], old_cache, queries, new_kv)
    ))


def solution(mesh):
    return jax.shard_map(
        on_device,
        mesh=mesh,
        in_specs=(
            P("inst", "group", None, None),
            P(),
            P(),
            P(),
            P(("group", "inst"), None),
            P(("group", "inst"), None),
        ),
        out_specs=P(("group", "inst"), None),
        check_vma=False,
    )
```

time: 129 us -> 120 us (0.930); the launches traced: 127 us -> 120 us
  other arithmetic: 2.86 us -> 0 us
  local copies, waits for them, and re-layouts: 3.19 us -> 0.97 us
  Pallas kernels: 121 us -> 119 us
    pallas_call x1, Pallas kernels: 121 us -> 119 us  [on_device(): pl.pallas_call(functools.partial(body, ngroup, ninst), out_shape=jax.Shap...]
    mul x1 -> x0, other arithmetic: 1.34 us -> none  [tables(): keys = (place_after[:, None] * per_inst + kk).reshape(1, -1)]
    unnamed x3 -> x1, local copies, waits for them, and re-layouts: 2.29 us -> 0.97 us
where the time goes in v3:
time: 120 us
  Pallas kernels  119 us (99%)
    pallas_call x1, Pallas kernels, on_device(): pl.pallas_call(functools.partial(body, ngroup, ninst), out_shape=jax.Shap...  119 us

profile of v3, /device:TPU:2, one launch (start us, length us, event | category | flops | bytes accessed | tf_op | source)
XLA Modules:
  0.0 120.2 jit_solution(15127916387928729590)
XLA Ops:
  0.0 119.2 %shard_map.64 = bf16[128,4096]{1,0:T(8,128)(2,1)S(1)} custom-call(s32[128,128]{1,0:T(8,128)} %blocks_hbm.1, s32[1,128]{1,0:T(1,128)} %bitcast.2, s32[1,128]{1,0:T(1,128)} %bitcast.3, bf16[1,64,16,2048]{3,2,1,0:T(8,128)(2,1)} %cache_hbm.1, bf16[128,4096]{1,0:T(8,128)(2,1)} %q.1, bf16[128,2048]{1,0:T(8,128)(2,1)} %kv.1), custom_call_target="tpu_custom_call" | custom-call | tf_op jit(solution)/shard_map/pallas_call | solution.py:372
  119.2 1.0 copy.8

commit v4 on v3

--- a/solution.py
+++ b/solution.py
@@ -252,6 +252,12 @@
     lane = lax.broadcasted_iota(jnp.int32, (tok, HD), 1)
     rb = 2 * tok
     ones = jnp.ones((ctx, HD), jnp.bfloat16)
+
+    def opart(c, b):
+        return to_partner(oo.at[c, b], orecv.at[c, b], osem.at[c, b], orsem.at[c, b])
+
+    def tpart(c):
+        return to_partner(st.at[c], strecv.at[c], tsem.at[c], trsem.at[c])
 
     def scores(c):
         for h in range(2):
@@ -297,31 +303,28 @@
                 if h == 1:
                     own[lax.rem(c, 2), at] = o[part]
                 else:
-                    oo[c, at] = o[part].astype(jnp.bfloat16)
+                    oo[c, b, j] = o[part].astype(jnp.bfloat16)
+            if h == 0 and b == 0:
+                opart(c, 0).start()
         if h == 1:
             stat[lax.rem(c, 2)] = stats
         else:
             st[c] = jnp.transpose(stats)[: 2 * groups]
 
-    def opart(c):
-        return to_partner(oo.at[c], orecv.at[c], osem.at[c], orsem.at[c])
-
-    def tpart(c):
-        return to_partner(st.at[c], strecv.at[c], tsem.at[c], trsem.at[c])
-
     def combine(c):
-        opart(c).wait_recv()
         tpart(c).wait_recv()
         fill = jnp.zeros((tok - 2 * groups, HD), jnp.float32)
         theirs = jnp.transpose(jnp.concatenate([strecv[c], fill], axis=0))
         mine = stat[lax.rem(c, 2)]
         top = jnp.maximum(mine, theirs)
         for j in range(groups):
+            if j % 2 == 0:
+                opart(c, j // 2).wait_recv()
             a, b = slice(j, j + 1), slice(groups + j, groups + j + 1)
             wa = mine[:, b] * jnp.exp2((mine[:, a] - top[:, a]) * COEF)
             wb = theirs[:, b] * jnp.exp2((theirs[:, a] - top[:, a]) * COEF)
             r = 1.0 / (wa + wb)
-            o = own[lax.rem(c, 2), j] * (wa * r) + orecv[c, j].astype(jnp.float32) * (wb * r)
+            o = own[lax.rem(c, 2), j] * (wa * r) + orecv[c, j // 2, j % 2].astype(jnp.float32) * (wb * r)
             out[:, pl.ds(pl.multiple_of(c * qw + j * HD, HD), HD)] = o.astype(jnp.bfloat16)
 
     def attention(c, _):
@@ -331,7 +334,7 @@
         all2(c, 1).wait_recv()
         values(c, 0)
         tpart(c).start()
-        opart(c).start()
+        opart(c, 1).start()
         values(c, 1)
 
         @pl.when(c > 0)
@@ -349,7 +352,8 @@
         swap(c).wait_send()
         all2(c, 0).wait_send()
         all2(c, 1).wait_send()
-        opart(c).wait_send()
+        opart(c, 0).wait_send()
+        opart(c, 1).wait_send()
         tpart(c).wait_send()
         return 0
 
@@ -394,12 +398,12 @@
             pltpu.VMEM((2 * rows, HD), f32),
             pltpu.VMEM((2, groups, tok, HD), f32),
             pltpu.VMEM((2, tok, HD), f32),
-            pltpu.VMEM((KVH, groups, tok, HD), bf),
-            pltpu.VMEM((KVH, groups, tok, HD), bf),
+            pltpu.VMEM((KVH, 2, groups // 2, tok, HD), bf),
+            pltpu.VMEM((KVH, 2, groups // 2, tok, HD), bf),
             pltpu.VMEM((KVH, 2 * groups, HD), f32),
             pltpu.VMEM((KVH, 2 * groups, HD), f32),
             dma((7,)), dma((len(PARTS),)), dma((len(PARTS),)), dma((KVH, 2)), dma((KVH, 2)),
-            dma((KVH,)), dma((KVH,)), dma((KVH,)), dma((KVH,)), dma((KVH,)), dma((KVH,)),
+            dma((KVH,)), dma((KVH,)), dma((KVH, 2)), dma((KVH, 2)), dma((KVH,)), dma((KVH,)),
         ],
         compiler_params=pltpu.CompilerParams(
             collective_id=0, has_side_effects=True, vmem_limit_bytes=VLIM * 1024 * 1024

time: 120 us -> 120 us (level)
  no operation moved by 1% of the time
where the time goes in v4:
time: 120 us
  Pallas kernels  119 us (99%)
    pallas_call x1, Pallas kernels, on_device(): pl.pallas_call(functools.partial(body, ngroup, ninst), out_shape=jax.Shap...  119 us

profile of v4, /device:TPU:2, one launch (start us, length us, event | category | flops | bytes accessed | tf_op | source)
XLA Modules:
  0.0 120.0 jit_solution(3079225345652194406)
XLA Ops:
  0.0 119.0 %shard_map.64 = bf16[128,4096]{1,0:T(8,128)(2,1)S(1)} custom-call(s32[128,128]{1,0:T(8,128)} %blocks_hbm.1, s32[1,128]{1,0:T(1,128)} %bitcast.2, s32[1,128]{1,0:T(1,128)} %bitcast.3, bf16[1,64,16,2048]{3,2,1,0:T(8,128)(2,1)} %cache_hbm.1, bf16[128,4096]{1,0:T(8,128)(2,1)} %q.1, bf16[128,2048]{1,0:T(8,128)(2,1)} %kv.1), custom_call_target="tpu_custom_call" | custom-call | tf_op jit(solution)/shard_map/pallas_call | solution.py:376
  119.1 1.0 copy.8

commit v5 on v4

--- a/solution.py
+++ b/solution.py
@@ -344,7 +344,6 @@
         return 0
 
     lax.fori_loop(0, KVH, attention, 0)
-    combine(KVH - 1)
     for p in range(parts):
         all1(p).wait_send()
 
@@ -352,12 +351,18 @@
         swap(c).wait_send()
         all2(c, 0).wait_send()
         all2(c, 1).wait_send()
+        tpart(c).wait_send()
+        return 0
+
+    lax.fori_loop(0, KVH, finish, 0)
+    combine(KVH - 1)
+
+    def finish_parts(c, _):
         opart(c, 0).wait_send()
         opart(c, 1).wait_send()
-        tpart(c).wait_send()
         return 0
 
-    lax.fori_loop(0, KVH, finish, 0)
+    lax.fori_loop(0, KVH, finish_parts, 0)
 
 
 def on_device(old_cache, block_table, place_after, context_len, queries, new_kv):

time: 120 us -> 120 us (level)
  no operation moved by 1% of the time
where the time goes in v5:
time: 120 us
  Pallas kernels  119 us (99%)
    pallas_call x1, Pallas kernels, on_device(): pl.pallas_call(functools.partial(body, ngroup, ninst), out_shape=jax.Shap...  119 us

profile of v5, /device:TPU:2, one launch (start us, length us, event | category | flops | bytes accessed | tf_op | source)
XLA Modules:
  0.0 120.0 jit_solution(11552672333020297233)
XLA Ops:
  0.0 119.0 %shard_map.64 = bf16[128,4096]{1,0:T(8,128)(2,1)S(1)} custom-call(s32[128,128]{1,0:T(8,128)} %blocks_hbm.1, s32[1,128]{1,0:T(1,128)} %bitcast.2, s32[1,128]{1,0:T(1,128)} %bitcast.3, bf16[1,64,16,2048]{3,2,1,0:T(8,128)(2,1)} %cache_hbm.1, bf16[128,4096]{1,0:T(8,128)(2,1)} %q.1, bf16[128,2048]{1,0:T(8,128)(2,1)} %kv.1), custom_call_target="tpu_custom_call" | custom-call | tf_op jit(solution)/shard_map/pallas_call | solution.py:381
  119.0 1.0 copy.8
